TPU v7x, 32 devices: a whole 2x2x4 slice. The times are simulated.
32 devices in a mesh: member: 2 (over core), section: 4 (over y, x), atoms: 4 (over z).
Axes of the slice: x: 2, y: 2, z: 4, core: 2. Of those that a mesh axis runs over, the one named last changes fastest.
Arguments:
- positions: float32 [8, 3, 512], P(None, None, 'atoms'), may hold values from -8 to 8
- atom_types: int32 [8, 512], P(None, 'atoms'), may hold values from 0 to 127
- neighbors: int32 [8, 512, 128], P(None, 'atoms'), may hold values from 0 to 511
- nbr_mask: int32 [8, 512, 128], P(None, 'atoms'), may hold values 0 or 1
- type_table: bfloat16 [2, 128, 128], P('member'), may hold values from -6 to 6
- norm_gain: bfloat16 [2, 4, 128], P('member', 'section'), may hold values from 0.25 to 1.75
- proj_weight: bfloat16 [2, 4, 128, 384], P('member', 'section'), may hold values from -0.5 to 0.5
- out_weight: bfloat16 [2, 4, 128, 128], P('member', 'section'), may hold values from -0.5 to 0.5
- force_coef: bfloat16 [2, 4, 4], P('member', 'section'), may hold values from -48 to 48
Outputs:
- atom_dev: float32 [8, 512], P('section', 'atoms')
- max_dev: float32 [8], P('section')
- mean_force: float32 [8, 3, 512], P('section', None, 'atoms')
Inputs may be any that keep to these rules, and one draw needn't show every extreme that they name: `neighbors`: indices of atoms of the same frame, repeats and the atom itself allowed.
All inputs are finite; a program needn't handle non-finite values. No bound on the sum of `nbr_mask` on one device may be relied on, other than what follows from the above.
Results may differ from a plain program's by a relative error of at most 0.013.
Values may be sent and summed in bfloat16 or wider, within the bound.
No kernel may reach another device: no remote copies, remote signals or barrier semaphores. Data moves between devices by JAX's collectives and lax.ppermute only.
A program may use at most 64 MiB of HBM per device.

v0:
```python
import math
import jax
import jax.numpy as jnp
from jax import lax
from jax.sharding import PartitionSpec as P


def geometry(nbr, mask, pos_all, pos_own):
    total_atoms = pos_all.shape[1]
    hit = (nbr[:, :, None] == lax.iota(jnp.int32, total_atoms)[None, None, :]).astype(jnp.float32)
    counts = jnp.sum(hit * mask.astype(jnp.float32)[:, :, None], 1)
    delta = pos_all[:, None, :] - pos_own[:, :, None]
    switch = 1.0 / (1.0 + 0.125 * jnp.sum(delta * delta, 0))
    return (counts * switch, delta)


def block_dev(h_in, gain, proj, outw, coef, pair, delta, slots):
    width = h_in.shape[1]
    heads = coef.shape[0]
    head_dim = width // heads
    count = h_in.shape[0]
    hf = h_in.astype(jnp.float32)
    normed = (
        hf * lax.rsqrt(jnp.mean(hf * hf, -1, keepdims=True) + 1e-06) * gain.astype(jnp.float32)
    ).astype(jnp.bfloat16)
    query = jnp.dot(normed, proj[:, :width], preferred_element_type=jnp.float32).astype(
        jnp.bfloat16
    )
    keyval = jnp.dot(
        lax.all_gather(normed, "atoms", axis=0, tiled=True),
        proj[:, width:],
        preferred_element_type=jnp.float32,
    ).astype(jnp.bfloat16)
    total_atoms = keyval.shape[0]
    query3 = query.reshape(count, heads, head_dim)
    keys = keyval[:, :width].reshape(total_atoms, heads, head_dim)
    values = keyval[:, width:].reshape(total_atoms, heads, head_dim)
    scores = jnp.einsum(
        "ahd,jhd->haj", query3, keys, preferred_element_type=jnp.float32
    ) / math.sqrt(head_dim)
    weights = jax.nn.sigmoid(scores) * pair[None]
    message = jnp.einsum(
        "haj,jhd->ahd", weights.astype(jnp.bfloat16), values, preferred_element_type=jnp.float32
    )
    message = (message / slots).reshape(count, width).astype(jnp.bfloat16)
    h_out = (hf + jnp.dot(message, outw, preferred_element_type=jnp.float32)).astype(jnp.bfloat16)
    pair_coef = jnp.einsum("h,haj->aj", coef.astype(jnp.float32), weights)
    force = jnp.einsum("aj,caj->ca", pair_coef, delta) / slots
    return (h_out, force)


def embed(types_now, table):
    onehot = (types_now[:, None] == lax.iota(jnp.int32, table.shape[0])[None, :]).astype(
        jnp.bfloat16
    )
    return jnp.dot(onehot, table, preferred_element_type=jnp.float32).astype(jnp.bfloat16)


def shards(
    positions,
    atom_types,
    neighbors,
    nbr_mask,
    type_table,
    norm_gain,
    proj_weight,
    out_weight,
    force_coef,
):
    n_section = lax.axis_size("section")
    section_idx = lax.axis_index("section")
    frames = atom_types.shape[0]
    per_section = frames // n_section
    count = atom_types.shape[1]
    slots = neighbors.shape[2]
    table = type_table[0]
    pos_all = lax.all_gather(positions, "atoms", axis=2, tiled=True)
    gains, projs, outs, coefs = (
        lax.all_gather(norm_gain, "section", axis=1, tiled=True),
        lax.all_gather(proj_weight, "section", axis=1, tiled=True),
        lax.all_gather(out_weight, "section", axis=1, tiled=True),
        lax.all_gather(force_coef, "section", axis=1, tiled=True),
    )
    first = section_idx * per_section

    def whole_frame(local, own_forces):
        frame = first + local
        nbr = lax.dynamic_index_in_dim(neighbors, frame, 0, keepdims=False)
        mask = lax.dynamic_index_in_dim(nbr_mask, frame, 0, keepdims=False)
        pos_now = lax.dynamic_index_in_dim(pos_all, frame, 0, keepdims=False)
        pos_own = lax.dynamic_index_in_dim(positions, frame, 0, keepdims=False)
        pair, delta = geometry(nbr, mask, pos_now, pos_own)
        h_cur = embed(lax.dynamic_index_in_dim(atom_types, frame, 0, keepdims=False), table)
        total = jnp.zeros((3, count), jnp.float32)
        for blk in range(n_section):
            h_cur, term = block_dev(
                h_cur, gains[0, blk], projs[0, blk], outs[0, blk], coefs[0, blk], pair, delta, slots
            )
            total = total + term
        return lax.dynamic_update_index_in_dim(own_forces, total, local, 0)

    own = lax.fori_loop(
        0, per_section, whole_frame, jnp.zeros((per_section, 3, count), jnp.float32)
    )
    members = lax.axis_size("member")
    mean_force = lax.psum(own, "member") / members
    centered = own - mean_force
    spread = lax.psum(jnp.sum(centered * centered, 1), "member") / members
    atom_dev = jnp.sqrt(spread)
    max_dev = lax.pmax(jnp.max(atom_dev, -1), "atoms")
    return (atom_dev, max_dev, mean_force)


def solution(mesh):
    return jax.shard_map(
        shards,
        mesh=mesh,
        in_specs=(
            P(None, None, "atoms"),
            P(None, "atoms"),
            P(None, "atoms", None),
            P(None, "atoms", None),
            P("member", None, None),
            P("member", "section", None),
            P("member", "section", None, None),
            P("member", "section", None, None),
            P("member", "section", None),
        ),
        out_specs=(P("section", "atoms"), P("section"), P("section", None, "atoms")),
        check_vma=False,
    )
```

profile of v0, /device:TPU:0, one launch (start us, length us, event | category | flops | bytes accessed | tf_op | source)
XLA Modules:
  0.0 200.3 jit_solution(8612434693529792498)
XLA Ops:
  0.6 9.5 %all_gather.44 = bf16[1,4,128]{2,0,1:T(2,128)(2,1)S(1)} all-gather(bf16[1,1,128]{2,0,1:T(2,128)(2,1)} %bitcast.301), channel_id=1, replica_groups=mesh['member'=2,'section'=4,'atoms'=4] {'section'}, dimensions={1}, use_global_device_ids=true | all-gather | bytes 1280 | tf_op jit(solution)/shard_map/all_gather | solution.py:79
  10.2 7.8 %all_gather.46 = bf16[1,4,4]{2,0,1:T(2,128)(2,1)S(1)} all-gather(bf16[1,1,4]{2,0,1:T(2,128)(2,1)} %bitcast.302), channel_id=1, replica_groups=mesh['member'=2,'section'=4,'atoms'=4] {'section'}, dimensions={1}, use_global_device_ids=true | all-gather | bytes 40 | tf_op jit(solution)/shard_map/all_gather | solution.py:82
  18.0 0.7 copy.31
  18.7 12.2 %all_gather.43 = f32[8,3,512]{2,1,0:T(4,128)S(1)} all-gather(f32[8,3,128]{2,1,0:T(4,128)S(1)} %copy.31), channel_id=1, replica_groups=mesh['member'=2,'section'=4,'atoms'=4] {'atoms'}, dimensions={2}, use_global_device_ids=true | all-gather | bytes 61440 | tf_op jit(solution)/shard_map/all_gather | solution.py:77
  30.9 7.7 %all_gather.47 = bf16[1,4,128,128]{3,2,0,1:T(8,128)(2,1)S(1)} all-gather(bf16[1,1,128,128]{3,2,0,1:T(8,128)(2,1)} %bitcast.300), channel_id=1, replica_groups=mesh['member'=2,'section'=4,'atoms'=4] {'section'}, dimensions={1}, use_global_device_ids=true | all-gather | bytes 163840 | tf_op jit(solution)/shard_map/all_gather | solution.py:81
  38.6 9.3 %all_gather.45 = bf16[1,4,128,384]{3,2,0,1:T(8,128)(2,1)S(1)} all-gather(bf16[1,1,128,384]{3,2,0,1:T(8,128)(2,1)} %bitcast.299), channel_id=1, replica_groups=mesh['member'=2,'section'=4,'atoms'=4] {'section'}, dimensions={1}, use_global_device_ids=true | all-gather | bytes 491520 | tf_op jit(solution)/shard_map/all_gather | solution.py:80
  47.9 137.4 %while.13 = (s32[]{:T(128)}, f32[2,3,128]{2,0,1:T(2,128)S(1)}, s32[]{:T(128)}, f32[8,3,512]{2,1,0:T(4,128)S(1)}, f32[8,3,128]{2,1,0:T(4,128)S(1)}, /*index=5*/s3...) while((s32[]{:T(128)}, f32[2,3,128]{2,0,1:T(2,128)S(1)}, ...), condition=%wide.region_7.8_spmd, body=%wide.region_0.7_spmd.sunk | while | flops 322554368 | bytes 20396256 | solution.py:102
  47.9 0.7 fusion.231
  49.0 0.9 convert_bitcast_fusion.2
  49.9 6.0 %select_reduce_fusion.2 = f32[128,512]{1,0:T(8,128)S(1)} fusion(f32[128,128]{1,0:T(8,128)S(1)} %get-tuple-element.420, s32[128,128]{1,0:T(8,128)S(1)} %get-tuple-element.421), kind=kLoop, calls=%fused_computation.clone.1 | loop fusion | flops 25100288 | bytes 393216 | tf_op jit(solution)/shard_map/while/body/eval_jaxpr/reduce_sum | solution.py:11
  55.8 12.3 %all_gather.52 = bf16[512,128]{0,1:T(8,128)(2,1)S(1)} all-gather(bf16[128,128]{0,1:T(8,128)(2,1)S(1)} %multiply_convert_fusion.8), channel_id=1, replica_groups=mesh['member'=2,'section'=4,'atoms'=4] {'atoms'}, dimensions={0}, use_global_device_ids=true | all-gather | bytes 163840 | tf_op jit(solution)/shard_map/while/body/eval_jaxpr/all_gather | solution.py:30
  69.7 0.5 fusion.249
  70.3 0.6 fusion.250
  71.6 12.3 %all_gather.53 = bf16[512,128]{0,1:T(8,128)(2,1)S(1)} all-gather(bf16[128,128]{0,1:T(8,128)(2,1)S(1)} %multiply_convert_fusion.9), channel_id=1, replica_groups=mesh['member'=2,'section'=4,'atoms'=4] {'atoms'}, dimensions={0}, use_global_device_ids=true | all-gather | bytes 163840 | tf_op jit(solution)/shard_map/while/body/eval_jaxpr/all_gather | solution.py:30
  84.1 0.5 fusion.236
  84.9 0.5 fusion.247
  85.5 0.6 fusion.248
  86.8 12.3 %all_gather.54 = bf16[512,128]{0,1:T(8,128)(2,1)S(1)} all-gather(bf16[128,128]{0,1:T(8,128)(2,1)S(1)} %multiply_convert_fusion.10), channel_id=1, replica_groups=mesh['member'=2,'section'=4,'atoms'=4] {'atoms'}, dimensions={0}, use_global_device_ids=true | all-gather | bytes 163840 | tf_op jit(solution)/shard_map/while/body/eval_jaxpr/all_gather | solution.py:30
  99.3 0.5 fusion.239
  100.1 0.5 fusion.245
  100.6 0.6 fusion.246
  101.9 12.5 %all_gather.55 = bf16[512,128]{0,1:T(8,128)(2,1)S(1)} all-gather(bf16[128,128]{0,1:T(8,128)(2,1)S(1)} %multiply_convert_fusion.11), channel_id=1, replica_groups=mesh['member'=2,'section'=4,'atoms'=4] {'atoms'}, dimensions={0}, use_global_device_ids=true | all-gather | bytes 163840 | tf_op jit(solution)/shard_map/while/body/eval_jaxpr/all_gather | solution.py:30
  114.7 0.5 fusion.242
  115.2 0.5 fusion.243
  115.7 0.6 fusion.244
  116.5 0.7 fusion.231
  117.6 0.9 convert_bitcast_fusion.2
  118.5 6.0 %select_reduce_fusion.2 = f32[128,512]{1,0:T(8,128)S(1)} fusion(f32[128,128]{1,0:T(8,128)S(1)} %get-tuple-element.420, s32[128,128]{1,0:T(8,128)S(1)} %get-tuple-element.421), kind=kLoop, calls=%fused_computation.clone.1 | loop fusion | flops 25100288 | bytes 393216 | tf_op jit(solution)/shard_map/while/body/eval_jaxpr/reduce_sum | solution.py:11
  124.5 12.5 %all_gather.52 = bf16[512,128]{0,1:T(8,128)(2,1)S(1)} all-gather(bf16[128,128]{0,1:T(8,128)(2,1)S(1)} %multiply_convert_fusion.8), channel_id=1, replica_groups=mesh['member'=2,'section'=4,'atoms'=4] {'atoms'}, dimensions={0}, use_global_device_ids=true | all-gather | bytes 163840 | tf_op jit(solution)/shard_map/while/body/eval_jaxpr/all_gather | solution.py:30
  137.9 0.5 fusion.233
  138.7 0.5 fusion.249
  139.2 0.6 fusion.250
  140.5 12.4 %all_gather.53 = bf16[512,128]{0,1:T(8,128)(2,1)S(1)} all-gather(bf16[128,128]{0,1:T(8,128)(2,1)S(1)} %multiply_convert_fusion.9), channel_id=1, replica_groups=mesh['member'=2,'section'=4,'atoms'=4] {'atoms'}, dimensions={0}, use_global_device_ids=true | all-gather | bytes 163840 | tf_op jit(solution)/shard_map/while/body/eval_jaxpr/all_gather | solution.py:30
  153.2 0.5 fusion.236
  153.9 0.5 fusion.247
  154.5 0.6 fusion.248
  155.8 12.3 %all_gather.54 = bf16[512,128]{0,1:T(8,128)(2,1)S(1)} all-gather(bf16[128,128]{0,1:T(8,128)(2,1)S(1)} %multiply_convert_fusion.10), channel_id=1, replica_groups=mesh['member'=2,'section'=4,'atoms'=4] {'atoms'}, dimensions={0}, use_global_device_ids=true | all-gather | bytes 163840 | tf_op jit(solution)/shard_map/while/body/eval_jaxpr/all_gather | solution.py:30
  168.3 0.5 fusion.239
  169.1 0.5 fusion.245
  169.6 0.6 fusion.246
  170.9 12.3 %all_gather.55 = bf16[512,128]{0,1:T(8,128)(2,1)S(1)} all-gather(bf16[128,128]{0,1:T(8,128)(2,1)S(1)} %multiply_convert_fusion.11), channel_id=1, replica_groups=mesh['member'=2,'section'=4,'atoms'=4] {'atoms'}, dimensions={0}, use_global_device_ids=true | all-gather | bytes 163840 | tf_op jit(solution)/shard_map/while/body/eval_jaxpr/all_gather | solution.py:30
  184.0 0.5 fusion.243
  184.5 0.6 fusion.244
  185.3 2.5 %psum.14 = f32[2,3,128]{2,0,1:T(2,128)S(1)} all-reduce(f32[2,3,128]{2,0,1:T(2,128)S(1)} %get-tuple-element.217), channel_id=1, replica_groups=mesh['member'=2,'section'=4,'atoms'=4] {'member'}, use_global_device_ids=true, to_apply=%region_8.9 | all-reduce | flops 768 | bytes 6144 | tf_op jit(solution)/shard_map/psum | solution.py:106
  187.8 0.6 multiply_reduce_fusion.5
  188.3 2.4 %psum.15 = f32[2,128]{1,0:T(2,128)S(1)} all-reduce(f32[2,128]{1,0:T(2,128)S(1)} %get-tuple-element.285), channel_id=1, replica_groups=mesh['member'=2,'section'=4,'atoms'=4] {'member'}, use_global_device_ids=true, to_apply=%region_10.11 | all-reduce | flops 256 | bytes 2048 | tf_op jit(solution)/shard_map/psum | solution.py:108
  190.8 0.7 fusion.80
  191.5 8.9 %pmax.7 = f32[2]{0:T(128)} all-reduce(f32[2]{0:T(128)S(1)} %get-tuple-element.283), channel_id=1, replica_groups=mesh['member'=2,'section'=4,'atoms'=4] {'atoms'}, use_global_device_ids=true, to_apply=%region_12.13 | all-reduce | flops 2 | bytes 16 | tf_op jit(solution)/shard_map/pmax | solution.py:110
  (97 shorter events, 10.9 us)
Async XLA Ops:
  0.6 47.2 %copy-start = (bf16[1,128,128]{2,1,0:T(8,128)(2,1)S(1)}, bf16[1,128,128]{2,1,0:T(8,128)(2,1)}, u32[]{:S(2)}) copy-start(bf16[1,128,128]{2,1,0:T(8,128)(2,1)} %param.15) | copy-start | bytes 98308
where the time goes:
time: 201 us; the launch traced here: 200 us
  blocking collectives  159 us (79%)
  matrix products  20.5 us (10%)
  other arithmetic  16.4 us (8%)
  local copies, waits for them, and re-layouts  3.21 us (2%)
    all_gather x8, blocking collectives, block_dev(): lax.all_gather(normed, 'atoms', axis=0, tiled=True)  98.7 us
    all_gather x1, blocking collectives, shards(): pos_all = lax.all_gather(positions, 'atoms', axis=2, tiled=True)  12.2 us
    reduce_sum x2, other arithmetic, geometry(): counts = jnp.sum(hit * mask.astype(jnp.float32)[:, :, None], 1)  11.9 us
    all_gather x1, blocking collectives, shards(): lax.all_gather(norm_gain, 'section', axis=1, tiled=True)  9.53 us
    all_gather x1, blocking collectives, shards(): lax.all_gather(proj_weight, 'section', axis=1, tiled=True)  9.27 us
    pmax x1, blocking collectives, shards(): max_dev = lax.pmax(jnp.max(atom_dev, -1), 'atoms')  8.87 us
    all_gather x1, blocking collectives, shards(): lax.all_gather(force_coef, 'section', axis=1, tiled=True)  7.81 us
    all_gather x1, blocking collectives, shards(): lax.all_gather(out_weight, 'section', axis=1, tiled=True)  7.68 us

commit v1 on v0

--- a/solution.py
+++ b/solution.py
@@ -74,7 +74,7 @@
     count = atom_types.shape[1]
     slots = neighbors.shape[2]
     table = type_table[0]
-    pos_all = lax.all_gather(positions, "atoms", axis=2, tiled=True)
+    pos_all = jnp.concatenate(lax.all_gather(positions, "atoms"), axis=2)
     gains, projs, outs, coefs = (
         lax.all_gather(norm_gain, "section", axis=1, tiled=True),
         lax.all_gather(proj_weight, "section", axis=1, tiled=True),

time: 201 us -> 203 us (level)
  no operation moved by 1% of the time
where the time goes in v1:
time: 203 us
  blocking collectives  160 us (79%)
  matrix products  20.5 us (10%)
  other arithmetic  16.4 us (8%)
  local copies, waits for them, and re-layouts  3.97 us (2%)
    all_gather x8, blocking collectives, block_dev(): lax.all_gather(normed, 'atoms', axis=0, tiled=True)  98.6 us
    all_gather x1, blocking collectives, shards(): pos_all = jnp.concatenate(lax.all_gather(positions, 'atoms'), axis=2)  13.6 us
    reduce_sum x2, other arithmetic, geometry(): counts = jnp.sum(hit * mask.astype(jnp.float32)[:, :, None], 1)  11.9 us
    all_gather x1, blocking collectives, shards(): lax.all_gather(norm_gain, 'section', axis=1, tiled=True)  9.66 us
    all_gather x1, blocking collectives, shards(): lax.all_gather(proj_weight, 'section', axis=1, tiled=True)  9.29 us
    pmax x1, blocking collectives, shards(): max_dev = lax.pmax(jnp.max(atom_dev, -1), 'atoms')  8.87 us
    all_gather x1, blocking collectives, shards(): lax.all_gather(force_coef, 'section', axis=1, tiled=True)  7.81 us
    all_gather x1, blocking collectives, shards(): lax.all_gather(out_weight, 'section', axis=1, tiled=True)  7.69 us

profile of v1, /device:TPU:0, one launch (start us, length us, event | category | flops | bytes accessed | tf_op | source)
XLA Modules:
  0.0 202.6 jit_solution(5075335206706424555)
XLA Ops:
  0.7 9.7 %all_gather.48 = bf16[1,4,128]{2,0,1:T(2,128)(2,1)S(1)} all-gather(bf16[1,1,128]{2,0,1:T(2,128)(2,1)} %bitcast.315), channel_id=1, replica_groups=mesh['member'=2,'section'=4,'atoms'=4] {'section'}, dimensions={1}, use_global_device_ids=true | all-gather | bytes 1280 | tf_op jit(solution)/shard_map/all_gather | solution.py:79
  10.3 7.8 %all_gather.50 = bf16[1,4,4]{2,0,1:T(2,128)(2,1)S(1)} all-gather(bf16[1,1,4]{2,0,1:T(2,128)(2,1)} %bitcast.316), channel_id=1, replica_groups=mesh['member'=2,'section'=4,'atoms'=4] {'section'}, dimensions={1}, use_global_device_ids=true | all-gather | bytes 40 | tf_op jit(solution)/shard_map/all_gather | solution.py:82
  18.1 13.6 %all-gather = f32[32,3,128]{2,0,1:T(8,128)S(1)} all-gather(f32[8,3,128]{2,0,1:T(8,128)} %param.11), channel_id=2, replica_groups=mesh['member'=2,'section'=4,'atoms'=4] {'atoms'}, dimensions={0}, use_global_device_ids=true | all-gather | bytes 61440 | tf_op jit(solution)/shard_map/all_gather | solution.py:77
  31.8 7.7 %all_gather.51 = bf16[1,4,128,128]{3,2,0,1:T(8,128)(2,1)S(1)} all-gather(bf16[1,1,128,128]{3,2,0,1:T(8,128)(2,1)} %bitcast.314), channel_id=1, replica_groups=mesh['member'=2,'section'=4,'atoms'=4] {'section'}, dimensions={1}, use_global_device_ids=true | all-gather | bytes 163840 | tf_op jit(solution)/shard_map/all_gather | solution.py:81
  39.5 9.3 %all_gather.49 = bf16[1,4,128,384]{3,2,0,1:T(8,128)(2,1)S(1)} all-gather(bf16[1,1,128,384]{3,2,0,1:T(8,128)(2,1)S(1)} %bitcast.313), channel_id=1, replica_groups=mesh['member'=2,'section'=4,'atoms'=4] {'section'}, dimensions={1}, use_global_device_ids=true | all-gather | bytes 491520 | tf_op jit(solution)/shard_map/all_gather | solution.py:80
  48.7 138.8 %while.13 = (s32[]{:T(128)}, f32[2,3,128]{2,0,1:T(2,128)S(1)}, s32[]{:T(128)}, f32[8,3,512]{2,0,1:T(8,128)S(1)}, f32[8,3,128]{2,0,1:T(8,128)}, /*index=5*/s32[8,...) while((s32[]{:T(128)}, f32[2,3,128]{2,0,1:T(2,128)S(1)}, ...), condition=%wide.region_7.8_spmd, body=%wide.region_0.7_spmd.sunk | while | flops 322554368 | bytes 20411616 | solution.py:102
  48.8 0.7 fusion.231
  49.5 0.7 constant_dynamic-slice_fusion.5
  50.6 0.9 convert_bitcast_fusion.2
  51.5 6.0 %select_reduce_fusion.2 = f32[128,512]{1,0:T(8,128)S(1)} fusion(f32[128,128]{1,0:T(8,128)S(1)} %get-tuple-element.420, s32[128,128]{1,0:T(8,128)S(1)} %get-tuple-element.421), kind=kLoop, calls=%fused_computation.clone.1 | loop fusion | flops 25100288 | bytes 393216 | tf_op jit(solution)/shard_map/while/body/eval_jaxpr/reduce_sum | solution.py:11
  57.4 12.3 %all_gather.56 = bf16[512,128]{0,1:T(8,128)(2,1)S(1)} all-gather(bf16[128,128]{0,1:T(8,128)(2,1)S(1)} %multiply_convert_fusion.8), channel_id=1, replica_groups=mesh['member'=2,'section'=4,'atoms'=4] {'atoms'}, dimensions={0}, use_global_device_ids=true | all-gather | bytes 163840 | tf_op jit(solution)/shard_map/while/body/eval_jaxpr/all_gather | solution.py:30
  70.6 0.5 fusion.233
  71.3 0.5 fusion.249
  71.9 0.6 fusion.250
  73.2 12.3 %all_gather.57 = bf16[512,128]{0,1:T(8,128)(2,1)S(1)} all-gather(bf16[128,128]{0,1:T(8,128)(2,1)S(1)} %multiply_convert_fusion.9), channel_id=1, replica_groups=mesh['member'=2,'section'=4,'atoms'=4] {'atoms'}, dimensions={0}, use_global_device_ids=true | all-gather | bytes 163840 | tf_op jit(solution)/shard_map/while/body/eval_jaxpr/all_gather | solution.py:30
  85.8 0.5 fusion.236
  86.6 0.5 fusion.247
  87.1 0.6 fusion.248
  88.4 12.3 %all_gather.58 = bf16[512,128]{0,1:T(8,128)(2,1)S(1)} all-gather(bf16[128,128]{0,1:T(8,128)(2,1)S(1)} %multiply_convert_fusion.10), channel_id=1, replica_groups=mesh['member'=2,'section'=4,'atoms'=4] {'atoms'}, dimensions={0}, use_global_device_ids=true | all-gather | bytes 163840 | tf_op jit(solution)/shard_map/while/body/eval_jaxpr/all_gather | solution.py:30
  101.0 0.5 fusion.239
  101.8 0.5 fusion.245
  102.3 0.6 fusion.246
  103.6 12.4 %all_gather.59 = bf16[512,128]{0,1:T(8,128)(2,1)S(1)} all-gather(bf16[128,128]{0,1:T(8,128)(2,1)S(1)} %multiply_convert_fusion.11), channel_id=1, replica_groups=mesh['member'=2,'section'=4,'atoms'=4] {'atoms'}, dimensions={0}, use_global_device_ids=true | all-gather | bytes 163840 | tf_op jit(solution)/shard_map/while/body/eval_jaxpr/all_gather | solution.py:30
  116.7 0.5 fusion.243
  117.3 0.6 fusion.244
  118.1 0.7 fusion.231
  118.8 0.7 constant_dynamic-slice_fusion.5
  119.9 0.9 convert_bitcast_fusion.2
  120.8 6.0 %select_reduce_fusion.2 = f32[128,512]{1,0:T(8,128)S(1)} fusion(f32[128,128]{1,0:T(8,128)S(1)} %get-tuple-element.420, s32[128,128]{1,0:T(8,128)S(1)} %get-tuple-element.421), kind=kLoop, calls=%fused_computation.clone.1 | loop fusion | flops 25100288 | bytes 393216 | tf_op jit(solution)/shard_map/while/body/eval_jaxpr/reduce_sum | solution.py:11
  126.7 12.3 %all_gather.56 = bf16[512,128]{0,1:T(8,128)(2,1)S(1)} all-gather(bf16[128,128]{0,1:T(8,128)(2,1)S(1)} %multiply_convert_fusion.8), channel_id=1, replica_groups=mesh['member'=2,'section'=4,'atoms'=4] {'atoms'}, dimensions={0}, use_global_device_ids=true | all-gather | bytes 163840 | tf_op jit(solution)/shard_map/while/body/eval_jaxpr/all_gather | solution.py:30
  139.9 0.5 fusion.233
  140.7 0.5 fusion.249
  141.2 0.6 fusion.250
  142.5 12.6 %all_gather.57 = bf16[512,128]{0,1:T(8,128)(2,1)S(1)} all-gather(bf16[128,128]{0,1:T(8,128)(2,1)S(1)} %multiply_convert_fusion.9), channel_id=1, replica_groups=mesh['member'=2,'section'=4,'atoms'=4] {'atoms'}, dimensions={0}, use_global_device_ids=true | all-gather | bytes 163840 | tf_op jit(solution)/shard_map/while/body/eval_jaxpr/all_gather | solution.py:30
  155.4 0.5 fusion.236
  156.1 0.5 fusion.247
  156.7 0.6 fusion.248
  158.0 12.3 %all_gather.58 = bf16[512,128]{0,1:T(8,128)(2,1)S(1)} all-gather(bf16[128,128]{0,1:T(8,128)(2,1)S(1)} %multiply_convert_fusion.10), channel_id=1, replica_groups=mesh['member'=2,'section'=4,'atoms'=4] {'atoms'}, dimensions={0}, use_global_device_ids=true | all-gather | bytes 163840 | tf_op jit(solution)/shard_map/while/body/eval_jaxpr/all_gather | solution.py:30
  171.3 0.5 fusion.245
  171.9 0.6 fusion.246
  173.2 12.3 %all_gather.59 = bf16[512,128]{0,1:T(8,128)(2,1)S(1)} all-gather(bf16[128,128]{0,1:T(8,128)(2,1)S(1)} %multiply_convert_fusion.11), channel_id=1, replica_groups=mesh['member'=2,'section'=4,'atoms'=4] {'atoms'}, dimensions={0}, use_global_device_ids=true | all-gather | bytes 163840 | tf_op jit(solution)/shard_map/while/body/eval_jaxpr/all_gather | solution.py:30
  186.2 0.5 fusion.243
  186.7 0.6 fusion.244
  187.5 2.5 %psum.14 = f32[2,3,128]{2,0,1:T(2,128)S(1)} all-reduce(f32[2,3,128]{2,0,1:T(2,128)S(1)} %get-tuple-element.217), channel_id=1, replica_groups=mesh['member'=2,'section'=4,'atoms'=4] {'member'}, use_global_device_ids=true, to_apply=%region_8.9 | all-reduce | flops 768 | bytes 6144 | tf_op jit(solution)/shard_map/psum | solution.py:106
  190.0 0.6 multiply_reduce_fusion.5
  190.6 2.4 %psum.15 = f32[2,128]{1,0:T(2,128)S(1)} all-reduce(f32[2,128]{1,0:T(2,128)S(1)} %get-tuple-element.285), channel_id=1, replica_groups=mesh['member'=2,'section'=4,'atoms'=4] {'member'}, use_global_device_ids=true, to_apply=%region_10.11 | all-reduce | flops 256 | bytes 2048 | tf_op jit(solution)/shard_map/psum | solution.py:108
  193.0 0.7 fusion.80
  193.7 8.9 %pmax.7 = f32[2]{0:T(128)} all-reduce(f32[2]{0:T(128)S(1)} %get-tuple-element.283), channel_id=1, replica_groups=mesh['member'=2,'section'=4,'atoms'=4] {'atoms'}, use_global_device_ids=true, to_apply=%region_12.13 | all-reduce | flops 2 | bytes 16 | tf_op jit(solution)/shard_map/pmax | solution.py:110
  (104 shorter events, 11.4 us)
Async XLA Ops:
  0.6 38.8 %copy-start.1 = (bf16[1,1,128,384]{3,2,1,0:T(8,128)(2,1)S(1)}, bf16[1,1,128,384]{3,2,1,0:T(8,128)(2,1)}, u32[]{:S(2)}) copy-start(bf16[1,1,128,384]{3,2,1,0:T(8,128)(2,1)} %param.17) | copy-start | bytes 294916
  0.6 48.1 %copy-start = (bf16[1,128,128]{2,1,0:T(8,128)(2,1)S(1)}, bf16[1,128,128]{2,1,0:T(8,128)(2,1)}, u32[]{:S(2)}) copy-start(bf16[1,128,128]{2,1,0:T(8,128)(2,1)} %param.15) | copy-start | bytes 98308
